TPU v7x, 128 devices: a whole 4x4x4 slice. The times are simulated.
128 devices in a mesh: tok: 16 (over z_lo, y, core), blk: 8 (over x, z_hi).
Axes of the slice: x: 4, y: 4, z: 4 (z_hi: 2, z_lo: 2; z = z_hi * 2 + z_lo), core: 2. Of those that a mesh axis runs over, the one named last changes fastest.
Arguments:
- activations: bfloat16 [8192, 4096], P('tok', 'blk'), may hold values from -52 to 52, as said below
- out_grads: bfloat16 [8192, 4096], P('tok', 'blk'), may hold values from -52 to 52, as said below
Outputs:
- act_inverse: float32 [4096, 4096], P(('tok', 'blk'))
- grad_inverse: float32 [4096, 4096], P(('tok', 'blk'))
Inputs may be any that keep to these rules, and one draw needn't show every extreme that they name: `activations`: real entries. `out_grads`: real entries.
All inputs are finite; a program needn't handle non-finite values.
Results may differ from a plain program's by a relative error of at most 0.02.
Values may be sent and summed in bfloat16 or wider, within the bound.
A program may use at most 64 MiB of HBM per device.

v0:
```python
import jax
import jax.numpy as jnp
from jax import lax
from jax.sharding import PartitionSpec as P

D = 4096
damping = 0.3
epsilon = 1e-06
divisor = 2.0


def laid_out(pieces, dim):
    pieces = jnp.moveaxis(pieces, 0, dim)
    dims = pieces.shape
    return pieces.reshape(*dims[:dim], dims[dim] * dims[dim + 1], *dims[dim + 2 :])


def sent_to_all(value, axis):
    length = lax.axis_size(axis)
    return lax.all_to_all(
        jnp.broadcast_to(value[None], (length, *value.shape)), axis, 0, 0, tiled=True
    )


def gather_directly(value, axis, dim):
    return laid_out(sent_to_all(value, axis), dim)


def side_by_side(arrays, axis, dim, along):
    widths = [a.shape[along] for a in arrays]
    both = jnp.concatenate(arrays, axis=along)
    out = lax.all_gather(both, axis, axis=dim, tiled=True)
    return tuple(jnp.split(out, [sum(widths[:k]) for k in range(1, len(widths))], axis=along))


def of_everyone(value, axis):
    everything = sent_to_all(value, axis)
    return jnp.sum(everything.astype(jnp.float32), axis=0)


def column_squares(data):
    values = data.astype(jnp.float32)
    return jnp.sum(values * values, axis=0)


def newton_steps(scaled, identity):
    half = scaled.astype(jnp.bfloat16)
    row_block = gather_directly(half, "blk", 1)
    column_block = lax.all_gather(half, "tok", axis=0, tiled=True)
    square = jnp.dot(row_block, column_block, preferred_element_type=jnp.float32)
    square_block = gather_directly(square.astype(jnp.bfloat16), "blk", 1)
    cube = jnp.dot(square_block, column_block, preferred_element_type=jnp.float32)
    return 4.0 * identity - 6.0 * scaled + 4.0 * square - cube


def body(activations, out_grads):
    tok_count = lax.axis_size("tok")
    blk_count = lax.axis_size("blk")
    tok_id = lax.axis_index("tok")
    blk_id = lax.axis_index("blk")
    token_count = activations.shape[0] * tok_count
    tile_rows = D // tok_count
    tile_cols = D // blk_count
    full_acts, full_grads = side_by_side((activations, out_grads), "blk", 1, 0)
    sums_act, sums_grad = (
        of_everyone(column_squares(full_acts).astype(jnp.bfloat16), "tok").astype(jnp.float32),
        of_everyone(column_squares(full_grads).astype(jnp.bfloat16), "tok").astype(jnp.float32),
    )
    row_ids = tok_id * tile_rows + jnp.arange(tile_rows, dtype=jnp.int32)
    col_ids = blk_id * tile_cols + jnp.arange(tile_cols, dtype=jnp.int32)
    identity = (row_ids[:, None] == col_ids[None, :]).astype(jnp.float32)

    def damped_tile(full, local, sums):
        gram_tile = lax.psum_scatter(
            lax.dot_general(
                full, local, (((0,), (0,)), ((), ())), preferred_element_type=jnp.float32
            ).astype(jnp.bfloat16),
            "tok",
            scatter_dimension=0,
            tiled=True,
        ).astype(jnp.float32)
        inverse = lax.rsqrt(sums / token_count + epsilon)
        inverse_rows = lax.dynamic_slice_in_dim(inverse, tok_id * tile_rows, tile_rows)
        inverse_cols = lax.dynamic_slice_in_dim(inverse, blk_id * tile_cols, tile_cols)
        return (
            gram_tile / token_count * inverse_rows[:, None] * inverse_cols[None, :]
            + damping * identity
        )

    damped_act = damped_tile(full_acts, activations, sums_act)
    damped_grad = damped_tile(full_grads, out_grads, sums_grad)
    results = []
    for damped in (damped_act, damped_grad):
        scaled = damped / divisor
        result_tile = newton_steps(scaled, identity)
        results.append(
            lax.all_to_all(
                result_tile.astype(jnp.bfloat16), "blk", split_axis=0, concat_axis=1, tiled=True
            ).astype(result_tile.dtype)
        )
    return (results[0], results[1])


def solution(mesh):
    placed = (P("tok", "blk"), P("tok", "blk"))
    return jax.shard_map(
        body,
        mesh=mesh,
        in_specs=placed,
        out_specs=(P(("tok", "blk"), None), P(("tok", "blk"), None)),
        check_vma=False,
    )
```

profile of v0, /device:TPU:0, one launch (start us, length us, event | category | flops | bytes accessed | tf_op | source)
XLA Modules:
  0.0 490.7 jit_solution(2053735657801038295)
XLA Ops:
  7.2 0.0 all-gather.4.cloned.1.call-start
  7.2 2.3 pad_maximum_fusion
  9.5 0.0 all-gather.4.cloned.1.call-update
  9.6 0.0 reduce-scatter.5.cloned.1.call-start
  9.6 122.6 %all-gather.4.cloned.1.call-done = bf16[1024,4096]{1,0:T(8,128)(2,1)} async-done(((bf16[1024,512]{1,0:T(8,128)(2,1)}), bf16[1024,4096]{1,0:T(8,128)(2,1)}) %all-gather.4.cloned.1.call-update) | async-done | bytes 8388624 | tf_op jit(solution)/shard_map/all_gather | solution.py:32
  132.2 6.7 %convolution_convert_fusion = bf16[4096,512]{1,0:T(8,128)(2,1)} fusion(bf16[512,512]{1,0:T(8,128)(2,1)} %param.3, bf16[1024,4096]{1,0:T(8,128)(2,1)} %all-gather.4.cloned.1.call-done), kind=kOutput, calls=%fused_computation.2 | convolution fusion | flops 2149580800 | bytes 8912896 | tf_op jit(solution)/shard_map/dot_general | solution.py:75
  138.9 0.0 reduce-scatter.5.cloned.1.call-update
  138.9 0.0 reduce-scatter.3.cloned.1.call-start
  139.0 1.0 copy-done.2
  139.9 6.5 %convolution_convert_fusion.1 = bf16[4096,512]{1,0:T(8,128)(2,1)} fusion(bf16[512,512]{1,0:T(8,128)(2,1)S(1)} %copy-done.2, bf16[1024,4096]{1,0:T(8,128)(2,1)} %all-gather.4.cloned.1.call-done), kind=kOutput, calls=%fused_computation.3 | convolution fusion | flops 2149580800 | bytes 8912896 | tf_op jit(solution)/shard_map/dot_general | solution.py:75
  146.5 4.4 multiply_reduce_fusion
  150.8 0.2 broadcast_in_dim.15
  151.0 0.5 broadcast.79
  151.6 1.4 reduce.2
  153.0 0.7 reshape.70
  153.7 4.7 all-to-all-start.4
  158.4 0.2 broadcast_in_dim.12
  158.6 1.4 reduce.3
  160.0 0.7 reshape.68
  160.8 4.1 all-to-all-done.4
  164.9 3.6 all-to-all-start
  168.5 0.0 all-gather.6.cloned.1.call-start
  168.5 0.1 reshape.71
  168.6 0.2 convert_reduce_fusion
  168.8 0.1 dynamic_slice.15
  168.9 6.4 %all-to-all-done = bf16[16,2,2048]{2,1,0:T(2,128)(2,1)S(1)} async-done(((bf16[16,2,2048]{2,1,0:T(2,128)(2,1)}), bf16[16,2,2048]{2,1,0:T(2,128)(2,1)S(1)}, u32[]{:S(2)}, u32[]{:S(2)}) %all-to-all-start) | async-done | bytes 131104 | tf_op jit(solution)/shard_map/all_to_all | solution.py:20
  175.3 0.1 reshape.69
  175.4 0.2 convert_reduce_fusion.1
  175.6 0.1 dynamic_slice.13
  175.7 0.1 dynamic-slice_multiply_fusion
  175.8 0.1 dynamic-slice_multiply_fusion.1
  175.9 31.3 %reduce-scatter.5.cloned.1.call-done = bf16[256,512]{1,0:T(8,128)(2,1)} async-done(((bf16[4096,512]{1,0:T(8,128)(2,1)}), bf16[256,512]{1,0:T(8,128)(2,1)}) %reduce-scatter.5.cloned.1.call-update) | async-done | bytes 262160 | tf_op jit(solution)/shard_map/reduce_scatter | solution.py:74
  207.1 67.9 %reduce-scatter.3.cloned.1.call-done = bf16[256,512]{1,0:T(8,128)(2,1)} async-done(((bf16[4096,512]{1,0:T(8,128)(2,1)}), bf16[256,512]{1,0:T(8,128)(2,1)}) %reduce-scatter.3.cloned.1.call-update) | async-done | bytes 262160 | tf_op jit(solution)/shard_map/reduce_scatter | solution.py:74
  275.0 2.1 multiply_convert_fusion
  277.1 0.0 all-gather.8.cloned.1.call-start
  277.2 0.5 all-gather.8.cloned.1.call-update
  277.7 1.1 copy.27
  278.8 1.5 broadcast_in_dim.13
  280.3 6.7 %all-to-all-start.1 = ((bf16[8,256,512]{1,2,0:T(8,128)(2,1)}), bf16[8,256,512]{1,2,0:T(8,128)(2,1)S(1)}, u32[]{:S(2)}, u32[]{:S(2)}) async-start(bf16[8,256,512]{1,2,0:T(8,128)(2,1)} %broadcast_in_dim.13), calls=%async_computation.2 | async-start | bytes 4194304 | tf_op jit(solution)/shard_map/all_to_all | solution.py:20
  287.1 0.1 copy.31
  287.2 29.2 %all-to-all-done.1 = bf16[8,256,512]{1,2,0:T(8,128)(2,1)S(1)} async-done(((bf16[8,256,512]{1,2,0:T(8,128)(2,1)}), bf16[8,256,512]{1,2,0:T(8,128)(2,1)S(1)}, u32[]{:S(2)}, u32[]{:S(2)}) %all-to-all-start.1) | async-done | bytes 2097184 | tf_op jit(solution)/shard_map/all_to_all | solution.py:20
  316.4 1.6 broadcast_in_dim.16
  318.0 0.4 copy-done.1
  318.4 4.7 all-to-all-start.5
  323.1 28.8 %all-gather.6.cloned.1.call-done = bf16[4096,512]{1,0:T(8,128)(2,1)} async-done(((bf16[256,512]{1,0:T(8,128)(2,1)}), bf16[4096,512]{1,0:T(8,128)(2,1)}) %all-gather.6.cloned.1.call-update) | async-done | bytes 4194320 | tf_op jit(solution)/shard_map/all_gather | solution.py:49
  351.9 4.1 fusion.8
  356.0 0.1 copy.28
  356.1 1.5 broadcast_in_dim.14
  357.6 7.7 %all-to-all-start.2 = ((bf16[8,256,512]{1,2,0:T(8,128)(2,1)}), bf16[8,256,512]{1,2,0:T(8,128)(2,1)}, u32[]{:S(2)}, u32[]{:S(2)}) async-start(bf16[8,256,512]{1,2,0:T(8,128)(2,1)} %broadcast_in_dim.14), calls=%async_computation.3 | async-start | bytes 4194304 | tf_op jit(solution)/shard_map/all_to_all | solution.py:20
  365.3 49.7 %all-gather.8.cloned.1.call-done = bf16[4096,512]{1,0:T(8,128)(2,1)} async-done(((bf16[256,512]{1,0:T(8,128)(2,1)}), bf16[4096,512]{1,0:T(8,128)(2,1)}) %all-gather.8.cloned.1.call-update) | async-done | bytes 4194320 | tf_op jit(solution)/shard_map/all_gather | solution.py:49
  415.0 4.2 fusion.9
  419.3 0.1 copy.32
  419.4 1.5 broadcast_in_dim.17
  420.9 6.8 %all-to-all-start.6 = ((bf16[8,256,512]{1,2,0:T(8,128)(2,1)}), bf16[8,256,512]{1,2,0:T(8,128)(2,1)S(1)}, u32[]{:S(2)}, u32[]{:S(2)}) async-start(bf16[8,256,512]{1,2,0:T(8,128)(2,1)} %broadcast_in_dim.17), calls=%async_computation.8 | async-start | bytes 4194304 | tf_op jit(solution)/shard_map/all_to_all | solution.py:20
  427.7 4.9 %fusion.2 = bf16[256,512]{1,0:T(8,128)(2,1)} fusion(bf16[256,4096]{0,1:T(8,128)(2,1)} %bitcast.3, bf16[4096,512]{1,0:T(8,128)(2,1)} %all-gather.6.cloned.1.call-done, f32[256,512]{1,0:T(8,128)S(1)} %get-tuple-element.7, bf16[256,512]{1,0:T(8,128)(2,1)S(1)} %copy-done.4, f32[512]{0:T(512)S(1)} %dynamic_slice.13, f32[256]{0:T(256)S(1)} %dynamic-slice_multiply_fusion.1, ...), kind=kOutput, calls=%fused_computation.8 | convolution fusion | flops 1075445760 | bytes 7346176 | tf_op jit(solution)/shard_map/dot_general | solution.py:52
  432.6 26.9 %all-to-all-done.6 = bf16[8,256,512]{1,2,0:T(8,128)(2,1)S(1)} async-done(((bf16[8,256,512]{1,2,0:T(8,128)(2,1)}), bf16[8,256,512]{1,2,0:T(8,128)(2,1)S(1)}, u32[]{:S(2)}, u32[]{:S(2)}) %all-to-all-start.6) | async-done | bytes 2097184 | tf_op jit(solution)/shard_map/all_to_all | solution.py:20
  459.5 3.5 all-to-all-start.3
  463.1 4.3 fusion.3
  467.4 4.1 all-to-all-done.3
  471.5 3.4 all-to-all-start.7
  474.9 0.1 convert_bitcast_fusion.1
  475.0 0.8 copy.34
  475.8 7.5 %all-to-all-done.7 = bf16[8,32,512]{2,1,0:T(8,128)(2,1)S(1)} async-done(((bf16[8,32,512]{2,1,0:T(8,128)(2,1)}), bf16[8,32,512]{2,1,0:T(8,128)(2,1)S(1)}, u32[]{:S(2)}, u32[]{:S(2)}) %all-to-all-start.7) | async-done | bytes 262176 | tf_op jit(solution)/shard_map/all_to_all | solution.py:97
  483.3 0.8 copy.35
  (17 shorter events, 0.1 us)
Async XLA Ops:
  7.2 125.1 %all-gather.4.cloned.1.call-start = ((), (), s32[]{:S(2)}) async-start(), calls=%async_computation.10 | async-start | bytes 9437184 | tf_op jit(solution)/shard_map/all_gather | solution.py:32
  9.6 197.6 %reduce-scatter.5.cloned.1.call-start = ((), (), s32[]{:S(2)}) async-start(), calls=%async_computation.13 | async-start | bytes 4456448 | tf_op jit(solution)/shard_map/reduce_scatter | solution.py:74
  138.9 1.0 copy-start.2
  138.9 136.1 %reduce-scatter.3.cloned.1.call-start = ((), (), s32[]{:S(2)}) async-start(), calls=%async_computation.11 | async-start | bytes 4456448 | tf_op jit(solution)/shard_map/reduce_scatter | solution.py:74
  153.7 11.2 %all-to-all-start.4 = ((bf16[16,2,2048]{2,1,0:T(2,128)(2,1)}), bf16[16,2,2048]{2,1,0:T(2,128)(2,1)S(1)}, u32[]{:S(2)}, u32[]{:S(2)}) async-start(bf16[16,2,2048]{2,1,0:T(2,128)(2,1)} %reshape.70), calls=%async_computation.6 | async-start | bytes 262144 | tf_op jit(solution)/shard_map/all_to_all | solution.py:20
  164.9 10.4 %all-to-all-start = ((bf16[16,2,2048]{2,1,0:T(2,128)(2,1)}), bf16[16,2,2048]{2,1,0:T(2,128)(2,1)S(1)}, u32[]{:S(2)}, u32[]{:S(2)}) async-start(bf16[16,2,2048]{2,1,0:T(2,128)(2,1)} %reshape.68), calls=%async_computation.1 | async-start | bytes 262144 | tf_op jit(solution)/shard_map/all_to_all | solution.py:20
  168.5 183.4 %all-gather.6.cloned.1.call-start = ((), (), s32[]{:S(2)}) async-start(), calls=%async_computation.12 | async-start | bytes 4456448 | tf_op jit(solution)/shard_map/all_gather | solution.py:49
  277.1 10.0 %copy-start = (bf16[256,512]{1,0:T(8,128)(2,1)S(1)}, bf16[256,512]{1,0:T(8,128)(2,1)}, u32[]{:S(2)}) copy-start(bf16[256,512]{1,0:T(8,128)(2,1)} %get-tuple-element.4) | copy-start | bytes 786436
  277.1 137.9 %all-gather.8.cloned.1.call-start = ((), (), s32[]{:S(2)}) async-start(), calls=%async_computation.14 | async-start | bytes 4456448 | tf_op jit(solution)/shard_map/all_gather | solution.py:49
  280.3 36.1 %all-to-all-start.1 = ((bf16[8,256,512]{1,2,0:T(8,128)(2,1)}), bf16[8,256,512]{1,2,0:T(8,128)(2,1)S(1)}, u32[]{:S(2)}, u32[]{:S(2)}) async-start(bf16[8,256,512]{1,2,0:T(8,128)(2,1)} %broadcast_in_dim.13), calls=%async_computation.2 | async-start | bytes 4194304 | tf_op jit(solution)/shard_map/all_to_all | solution.py:20
  316.4 2.0 copy-start.1
  318.4 37.7 %all-to-all-start.5 = ((bf16[8,256,512]{1,2,0:T(8,128)(2,1)}), bf16[8,256,512]{1,2,0:T(8,128)(2,1)S(1)}, u32[]{:S(2)}, u32[]{:S(2)}) async-start(bf16[8,256,512]{1,2,0:T(8,128)(2,1)} %broadcast_in_dim.16), calls=%async_computation.7 | async-start | bytes 4194304 | tf_op jit(solution)/shard_map/all_to_all | solution.py:20
  357.6 61.8 %all-to-all-start.2 = ((bf16[8,256,512]{1,2,0:T(8,128)(2,1)}), bf16[8,256,512]{1,2,0:T(8,128)(2,1)}, u32[]{:S(2)}, u32[]{:S(2)}) async-start(bf16[8,256,512]{1,2,0:T(8,128)(2,1)} %broadcast_in_dim.14), calls=%async_computation.3 | async-start | bytes 4194304 | tf_op jit(solution)/shard_map/all_to_all | solution.py:20
  419.2 8.5 %copy-start.4 = (bf16[256,512]{1,0:T(8,128)(2,1)S(1)}, bf16[256,512]{1,0:T(8,128)(2,1)}, u32[]{:S(2)}) copy-start(bf16[256,512]{1,0:T(8,128)(2,1)} %reduce-scatter.3.cloned.1.call-done) | copy-start | bytes 786436
  420.9 38.6 %all-to-all-start.6 = ((bf16[8,256,512]{1,2,0:T(8,128)(2,1)}), bf16[8,256,512]{1,2,0:T(8,128)(2,1)S(1)}, u32[]{:S(2)}, u32[]{:S(2)}) async-start(bf16[8,256,512]{1,2,0:T(8,128)(2,1)} %broadcast_in_dim.17), calls=%async_computation.8 | async-start | bytes 4194304 | tf_op jit(solution)/shard_map/all_to_all | solution.py:20
  427.7 35.3 %copy-start.3 = (bf16[256,512]{1,0:T(8,128)(2,1)S(1)}, bf16[256,512]{1,0:T(8,128)(2,1)}, u32[]{:S(2)}) copy-start(bf16[256,512]{1,0:T(8,128)(2,1)} %reduce-scatter.5.cloned.1.call-done) | copy-start | bytes 786436
  459.5 12.0 %all-to-all-start.3 = ((bf16[8,32,512]{2,1,0:T(8,128)(2,1)}), bf16[8,32,512]{2,1,0:T(8,128)(2,1)S(1)}, u32[]{:S(2)}, u32[]{:S(2)}) async-start(bf16[8,32,512]{2,1,0:T(8,128)(2,1)} %bitcast.4), calls=%async_computation.4 | async-start | bytes 524288 | tf_op jit(solution)/shard_map/all_to_all | solution.py:97
  471.5 11.8 %all-to-all-start.7 = ((bf16[8,32,512]{2,1,0:T(8,128)(2,1)}), bf16[8,32,512]{2,1,0:T(8,128)(2,1)S(1)}, u32[]{:S(2)}, u32[]{:S(2)}) async-start(bf16[8,32,512]{2,1,0:T(8,128)(2,1)} %bitcast.10), calls=%async_computation.9 | async-start | bytes 524288 | tf_op jit(solution)/shard_map/all_to_all | solution.py:97
Sparse Core Ops, SparseCore 0:
  10.2 122.0 all-gather.3
  139.1 68.0 reduce-scatter.4
  209.5 65.4 reduce-scatter.2
  277.3 74.5 all-gather.5
  354.0 60.9 all-gather.7
where the time goes:
time: 492 us; the launch traced here: 491 us
  waiting for transfers between devices  379 us (77%)
  starting transfers between devices  41.3 us (8%)
  matrix products  30.8 us (6%)
  between operations  14 us (3%)
  local copies, waits for them, and re-layouts  13.4 us (3%)
  other arithmetic  12.2 us (2%)
    all_gather x1, waiting for transfers between devices, side_by_side(): out = lax.all_gather(both, axis, axis=dim, tiled=True)  123 us
    reduce_scatter x2, waiting for transfers between devices, damped_tile(): lax.psum_scatter(lax.dot_general(full, local, (((0,), (0,)), ((), ())), p...  99.2 us
    all_gather x2, waiting for transfers between devices, newton_steps(): column_block = lax.all_gather(half, 'tok', axis=0, tiled=True)  78.5 us
    all_to_all x6, waiting for transfers between devices, sent_to_all(): lax.all_to_all(jnp.broadcast_to(value[None], (length, *value.shape)), axi...  66.5 us
    all_to_all x6, starting transfers between devices, sent_to_all(): lax.all_to_all(jnp.broadcast_to(value[None], (length, *value.shape)), axi...  34.2 us
    dot_general x2, matrix products, damped_tile(): lax.dot_general(full, local, (((0,), (0,)), ((), ())), preferred_element_...  13.2 us
    all_to_all x2, waiting for transfers between devices, body(): lax.all_to_all(result_tile.astype(jnp.bfloat16), 'blk', split_axis=0, con...  11.6 us
  transfers between devices with their start and end apart: 13, of which 11 were waited for; matrix products, arithmetic and copies ran while one was open for 8% of the time, Pallas kernels for 0%

commit v1 on v0

--- a/solution.py
+++ b/solution.py
@@ -46,7 +46,8 @@
 def newton_steps(scaled, identity):
     half = scaled.astype(jnp.bfloat16)
     row_block = gather_directly(half, "blk", 1)
-    column_block = lax.all_gather(half, "tok", axis=0, tiled=True)
+    sent = jnp.stack([half] * lax.axis_size("tok"))
+    column_block = jnp.concatenate(lax.all_to_all(sent, "tok", 0, 0), axis=0)
     square = jnp.dot(row_block, column_block, preferred_element_type=jnp.float32)
     square_block = gather_directly(square.astype(jnp.bfloat16), "blk", 1)
     cube = jnp.dot(square_block, column_block, preferred_element_type=jnp.float32)

time: 492 us -> 570 us (1.16)
  blocking collectives: 0 us -> 89.7 us
  starting transfers between devices: 41.3 us -> 34.8 us
  waiting for transfers between devices: 379 us -> 373 us
    all_to_all x0 -> x2, blocking collectives: none -> 89.7 us  [the longest x1 60.2 us: newton_steps(): column_block = jnp.concatenate(lax.all_to_all(sent, 'tok', 0, 0), axis=0)]
    all_gather x2 -> x0, waiting for transfers between devices: 78.5 us -> none  [newton_steps(): column_block = lax.all_gather(half, 'tok', axis=0, tiled=True)]
    all_to_all x0 -> x1, waiting for transfers between devices: none -> 50.8 us  [newton_steps(): column_block = jnp.concatenate(lax.all_to_all(sent, 'tok', 0, 0), axis=0)]
    all_to_all x6 -> x5, waiting for transfers between devices: 66.5 us -> 89 us  [sent_to_all(): lax.all_to_all(jnp.broadcast_to(value[None], (length, *value.shape)), axi...]
    all_to_all x6 -> x5, starting transfers between devices: 34.2 us -> 23.1 us  [sent_to_all(): lax.all_to_all(jnp.broadcast_to(value[None], (length, *value.shape)), axi...]
  transfers between devices with their start and end apart: 13 -> 11, of which waited for: 11 -> 11; matrix products, arithmetic and copies ran while one was open for 8% -> 6% of each run, Pallas kernels for 0% -> 0%
where the time goes in v1:
time: 570 us; the launch traced here: 568 us
  waiting for transfers between devices  373 us (65%)
  blocking collectives  89.7 us (16%)
  starting transfers between devices  34.8 us (6%)
  matrix products  30.7 us (5%)
  local copies, waits for them, and re-layouts  14.6 us (3%)
  between operations  14 us (2%)
  other arithmetic  11.3 us (2%)
    all_gather x1, waiting for transfers between devices, side_by_side(): out = lax.all_gather(both, axis, axis=dim, tiled=True)  123 us
    reduce_scatter x2, waiting for transfers between devices, damped_tile(): lax.psum_scatter(lax.dot_general(full, local, (((0,), (0,)), ((), ())), p...  99.2 us
    all_to_all x5, waiting for transfers between devices, sent_to_all(): lax.all_to_all(jnp.broadcast_to(value[None], (length, *value.shape)), axi...  89 us
    all_to_all x1, blocking collectives, newton_steps(): column_block = jnp.concatenate(lax.all_to_all(sent, 'tok', 0, 0), axis=0)  60.2 us
    all_to_all x1, waiting for transfers between devices, newton_steps(): column_block = jnp.concatenate(lax.all_to_all(sent, 'tok', 0, 0), axis=0)  50.8 us
    all_to_all x1, blocking collectives, sent_to_all(): lax.all_to_all(jnp.broadcast_to(value[None], (length, *value.shape)), axi...  29.5 us
    all_to_all x5, starting transfers between devices, sent_to_all(): lax.all_to_all(jnp.broadcast_to(value[None], (length, *value.shape)), axi...  23.1 us
    dot_general x2, matrix products, damped_tile(): lax.dot_general(full, local, (((0,), (0,)), ((), ())), preferred_element_...  13.2 us
  transfers between devices with their start and end apart: 11, of which 11 were waited for; matrix products, arithmetic and copies ran while one was open for 6% of the time, Pallas kernels for 0%

profile of v1, /device:TPU:0, one launch (start us, length us, event | category | flops | bytes accessed | tf_op | source)
XLA Modules:
  0.0 568.3 jit_solution(3822521726182024350)
XLA Ops:
  7.2 0.0 all-gather.2.cloned.1.call-start
  7.2 2.3 pad_maximum_fusion
  9.5 0.0 all-gather.2.cloned.1.call-update
  9.6 0.0 reduce-scatter.5.cloned.1.call-start
  9.6 122.6 %all-gather.2.cloned.1.call-done = bf16[1024,4096]{1,0:T(8,128)(2,1)} async-done(((bf16[1024,512]{1,0:T(8,128)(2,1)}), bf16[1024,4096]{1,0:T(8,128)(2,1)}) %all-gather.2.cloned.1.call-update) | async-done | bytes 8388624 | tf_op jit(solution)/shard_map/all_gather | solution.py:32
  132.2 6.7 %convolution_convert_fusion = bf16[4096,512]{1,0:T(8,128)(2,1)} fusion(bf16[512,512]{1,0:T(8,128)(2,1)} %param.3, bf16[1024,4096]{1,0:T(8,128)(2,1)} %all-gather.2.cloned.1.call-done), kind=kOutput, calls=%fused_computation.2 | convolution fusion | flops 2149580800 | bytes 8912896 | tf_op jit(solution)/shard_map/dot_general | solution.py:76
  138.9 0.0 reduce-scatter.5.cloned.1.call-update
  138.9 0.0 reduce-scatter.3.cloned.1.call-start
  139.0 1.0 copy-done.1
  139.9 6.5 %convolution_convert_fusion.1 = bf16[4096,512]{1,0:T(8,128)(2,1)} fusion(bf16[512,512]{1,0:T(8,128)(2,1)S(1)} %copy-done.1, bf16[1024,4096]{1,0:T(8,128)(2,1)} %all-gather.2.cloned.1.call-done), kind=kOutput, calls=%fused_computation.3 | convolution fusion | flops 2149580800 | bytes 8912896 | tf_op jit(solution)/shard_map/dot_general | solution.py:76
  146.5 4.4 multiply_reduce_fusion
  150.8 0.2 broadcast_in_dim.15
  151.0 0.5 broadcast.83
  151.5 1.4 reduce.2
  152.9 0.7 reshape.82
  153.7 4.7 all-to-all-start.5
  158.4 0.2 broadcast_in_dim.12
  158.6 1.4 reduce.3
  160.0 0.7 reshape.80
  160.7 4.1 all-to-all-done.5
  164.8 3.7 all-to-all-start
  168.5 0.1 reshape.83
  168.6 0.2 convert_reduce_fusion
  168.8 0.1 dynamic_slice.15
  168.9 6.5 %all-to-all-done = bf16[16,2,2048]{2,1,0:T(2,128)(2,1)S(1)} async-done(((bf16[16,2,2048]{2,1,0:T(2,128)(2,1)}), bf16[16,2,2048]{2,1,0:T(2,128)(2,1)S(1)}, u32[]{:S(2)}, u32[]{:S(2)}) %all-to-all-start) | async-done | bytes 131104 | tf_op jit(solution)/shard_map/all_to_all | solution.py:20
  175.4 0.1 reshape.81
  175.5 0.2 convert_reduce_fusion.1
  175.7 0.1 dynamic_slice.13
  175.8 0.1 dynamic-slice_multiply_fusion
  175.8 31.3 %reduce-scatter.5.cloned.1.call-done = bf16[256,512]{1,0:T(8,128)(2,1)} async-done(((bf16[4096,512]{1,0:T(8,128)(2,1)}), bf16[256,512]{1,0:T(8,128)(2,1)}) %reduce-scatter.5.cloned.1.call-update) | async-done | bytes 262160 | tf_op jit(solution)/shard_map/reduce_scatter | solution.py:75
  207.1 67.9 %reduce-scatter.3.cloned.1.call-done = bf16[256,512]{1,0:T(8,128)(2,1)} async-done(((bf16[4096,512]{1,0:T(8,128)(2,1)}), bf16[256,512]{1,0:T(8,128)(2,1)}) %reduce-scatter.3.cloned.1.call-update) | async-done | bytes 262160 | tf_op jit(solution)/shard_map/reduce_scatter | solution.py:75
  275.0 1.3 multiply_convert_fusion
  276.3 0.1 copy.27
  276.5 1.5 broadcast_in_dim.13
  277.9 6.7 %all-to-all-start.1 = ((bf16[8,256,512]{1,2,0:T(8,128)(2,1)}), bf16[8,256,512]{1,2,0:T(8,128)(2,1)S(1)}, u32[]{:S(2)}, u32[]{:S(2)}) async-start(bf16[8,256,512]{1,2,0:T(8,128)(2,1)} %broadcast_in_dim.13), calls=%async_computation.2 | async-start | bytes 4194304 | tf_op jit(solution)/shard_map/all_to_all | solution.py:20
  284.7 0.1 copy.31
  284.8 25.5 %all-to-all-done.1 = bf16[8,256,512]{1,2,0:T(8,128)(2,1)S(1)} async-done(((bf16[8,256,512]{1,2,0:T(8,128)(2,1)}), bf16[8,256,512]{1,2,0:T(8,128)(2,1)S(1)}, u32[]{:S(2)}, u32[]{:S(2)}) %all-to-all-start.1) | async-done | bytes 2097184 | tf_op jit(solution)/shard_map/all_to_all | solution.py:20
  310.4 1.3 copy-done
  311.7 0.1 broadcast_in_dim.16
  311.8 29.5 %all_to_all.68 = bf16[8,256,512]{1,2,0:T(8,128)(2,1)S(1)} all-to-all(bf16[8,256,512]{1,2,0:T(8,128)(2,1)S(1)} %broadcast_in_dim.16), channel_id=1, replica_groups=mesh['tok'=16,'blk'=8] {'blk'}, dimensions={0} | all-to-all | bytes 4194304 | tf_op jit(solution)/shard_map/all_to_all | solution.py:20
  341.3 0.4 stack.4
  341.7 60.2 %all_to_all.69 = bf16[16,256,512]{2,1,0:T(8,128)(2,1)} all-to-all(bf16[16,256,512]{2,1,0:T(8,128)(2,1)S(1)} %stack.4), channel_id=1, replica_groups=mesh['tok'=16,'blk'=8] {'tok'}, dimensions={0} | all-to-all | bytes 8388608 | tf_op jit(solution)/shard_map/all_to_all | solution.py:50
  402.0 2.4 stack.5
  404.3 4.7 all-to-all-start.7
  409.1 4.9 fusion.8
  414.0 0.1 copy.28
  414.1 50.8 %all-to-all-done.7 = bf16[16,256,512]{2,1,0:T(8,128)(2,1)} async-done(((bf16[16,256,512]{2,1,0:T(8,128)(2,1)}), bf16[16,256,512]{2,1,0:T(8,128)(2,1)}, u32[]{:S(2)}, u32[]{:S(2)}) %all-to-all-start.7) | async-done | bytes 4194336 | tf_op jit(solution)/shard_map/all_to_all | solution.py:50
  464.9 1.5 broadcast_in_dim.14
  466.3 4.4 all-to-all-start.3
  470.7 3.5 fusion.9
  474.2 0.1 copy.32
  474.4 27.8 %all-to-all-done.3 = bf16[8,256,512]{1,2,0:T(8,128)(2,1)} async-done(((bf16[8,256,512]{1,2,0:T(8,128)(2,1)}), bf16[8,256,512]{1,2,0:T(8,128)(2,1)}, u32[]{:S(2)}, u32[]{:S(2)}) %all-to-all-start.3) | async-done | bytes 2097184 | tf_op jit(solution)/shard_map/all_to_all | solution.py:20
  502.1 1.5 broadcast_in_dim.17
  503.6 3.6 all-to-all-start.8
  507.2 5.0 fusion.2
  512.2 25.1 %all-to-all-done.8 = bf16[8,256,512]{1,2,0:T(8,128)(2,1)S(1)} async-done(((bf16[8,256,512]{1,2,0:T(8,128)(2,1)}), bf16[8,256,512]{1,2,0:T(8,128)(2,1)S(1)}, u32[]{:S(2)}, u32[]{:S(2)}) %all-to-all-start.8) | async-done | bytes 2097184 | tf_op jit(solution)/shard_map/all_to_all | solution.py:20
  537.3 3.4 all-to-all-start.4
  540.7 4.2 fusion.3
  545.0 4.1 all-to-all-done.4
  549.1 3.4 all-to-all-start.9
  552.5 0.1 convert_bitcast_fusion.1
  552.6 0.8 copy.34
  553.4 7.5 %all-to-all-done.9 = bf16[8,32,512]{2,1,0:T(8,128)(2,1)S(1)} async-done(((bf16[8,32,512]{2,1,0:T(8,128)(2,1)}), bf16[8,32,512]{2,1,0:T(8,128)(2,1)S(1)}, u32[]{:S(2)}, u32[]{:S(2)}) %all-to-all-start.9) | async-done | bytes 262176 | tf_op jit(solution)/shard_map/all_to_all | solution.py:98
  561.0 0.8 copy.35
  (12 shorter events, 0.1 us)
Async XLA Ops:
  7.2 125.1 %all-gather.2.cloned.1.call-start = ((), (), s32[]{:S(2)}) async-start(), calls=%async_computation.12 | async-start | bytes 9437184 | tf_op jit(solution)/shard_map/all_gather | solution.py:32
  9.6 197.6 %reduce-scatter.5.cloned.1.call-start = ((), (), s32[]{:S(2)}) async-start(), calls=%async_computation.14 | async-start | bytes 4456448 | tf_op jit(solution)/shard_map/reduce_scatter | solution.py:75
  138.9 1.0 copy-start.1
  138.9 136.1 %reduce-scatter.3.cloned.1.call-start = ((), (), s32[]{:S(2)}) async-start(), calls=%async_computation.13 | async-start | bytes 4456448 | tf_op jit(solution)/shard_map/reduce_scatter | solution.py:75
  153.7 11.1 %all-to-all-start.5 = ((bf16[16,2,2048]{2,1,0:T(2,128)(2,1)}), bf16[16,2,2048]{2,1,0:T(2,128)(2,1)S(1)}, u32[]{:S(2)}, u32[]{:S(2)}) async-start(bf16[16,2,2048]{2,1,0:T(2,128)(2,1)} %reshape.82), calls=%async_computation.7 | async-start | bytes 262144 | tf_op jit(solution)/shard_map/all_to_all | solution.py:20
  164.8 10.6 %all-to-all-start = ((bf16[16,2,2048]{2,1,0:T(2,128)(2,1)}), bf16[16,2,2048]{2,1,0:T(2,128)(2,1)S(1)}, u32[]{:S(2)}, u32[]{:S(2)}) async-start(bf16[16,2,2048]{2,1,0:T(2,128)(2,1)} %reshape.80), calls=%async_computation.1 | async-start | bytes 262144 | tf_op jit(solution)/shard_map/all_to_all | solution.py:20
  277.9 32.4 %all-to-all-start.1 = ((bf16[8,256,512]{1,2,0:T(8,128)(2,1)}), bf16[8,256,512]{1,2,0:T(8,128)(2,1)S(1)}, u32[]{:S(2)}, u32[]{:S(2)}) async-start(bf16[8,256,512]{1,2,0:T(8,128)(2,1)} %broadcast_in_dim.13), calls=%async_computation.2 | async-start | bytes 4194304 | tf_op jit(solution)/shard_map/all_to_all | solution.py:20
  310.4 1.3 copy-start
  404.3 60.5 %all-to-all-start.7 = ((bf16[16,256,512]{2,1,0:T(8,128)(2,1)}), bf16[16,256,512]{2,1,0:T(8,128)(2,1)}, u32[]{:S(2)}, u32[]{:S(2)}) async-start(bf16[16,256,512]{2,1,0:T(8,128)(2,1)} %stack.5), calls=%async_computation.9 | async-start | bytes 8388608 | tf_op jit(solution)/shard_map/all_to_all | solution.py:50
  466.3 35.8 %all-to-all-start.3 = ((bf16[8,256,512]{1,2,0:T(8,128)(2,1)}), bf16[8,256,512]{1,2,0:T(8,128)(2,1)}, u32[]{:S(2)}, u32[]{:S(2)}) async-start(bf16[8,256,512]{1,2,0:T(8,128)(2,1)} %broadcast_in_dim.14), calls=%async_computation.4 | async-start | bytes 4194304 | tf_op jit(solution)/shard_map/all_to_all | solution.py:20
  474.2 33.0 %copy-start.3 = (bf16[256,512]{1,0:T(8,128)(2,1)S(1)}, bf16[256,512]{1,0:T(8,128)(2,1)}, u32[]{:S(2)}) copy-start(bf16[256,512]{1,0:T(8,128)(2,1)} %reduce-scatter.3.cloned.1.call-done) | copy-start | bytes 786436
  503.6 33.7 %all-to-all-start.8 = ((bf16[8,256,512]{1,2,0:T(8,128)(2,1)}), bf16[8,256,512]{1,2,0:T(8,128)(2,1)S(1)}, u32[]{:S(2)}, u32[]{:S(2)}) async-start(bf16[8,256,512]{1,2,0:T(8,128)(2,1)} %broadcast_in_dim.17), calls=%async_computation.10 | async-start | bytes 4194304 | tf_op jit(solution)/shard_map/all_to_all | solution.py:20
  507.2 33.5 %copy-start.2 = (bf16[256,512]{1,0:T(8,128)(2,1)S(1)}, bf16[256,512]{1,0:T(8,128)(2,1)}, u32[]{:S(2)}) copy-start(bf16[256,512]{1,0:T(8,128)(2,1)} %reduce-scatter.5.cloned.1.call-done) | copy-start | bytes 786436
  537.3 11.8 %all-to-all-start.4 = ((bf16[8,32,512]{2,1,0:T(8,128)(2,1)}), bf16[8,32,512]{2,1,0:T(8,128)(2,1)S(1)}, u32[]{:S(2)}, u32[]{:S(2)}) async-start(bf16[8,32,512]{2,1,0:T(8,128)(2,1)} %bitcast.5), calls=%async_computation.5 | async-start | bytes 524288 | tf_op jit(solution)/shard_map/all_to_all | solution.py:98
  549.1 11.8 %all-to-all-start.9 = ((bf16[8,32,512]{2,1,0:T(8,128)(2,1)}), bf16[8,32,512]{2,1,0:T(8,128)(2,1)S(1)}, u32[]{:S(2)}, u32[]{:S(2)}) async-start(bf16[8,32,512]{2,1,0:T(8,128)(2,1)} %bitcast.12), calls=%async_computation.11 | async-start | bytes 524288 | tf_op jit(solution)/shard_map/all_to_all | solution.py:98
Sparse Core Ops, SparseCore 0:
  10.2 122.0 all-gather.1
  139.0 68.0 reduce-scatter.4
  209.5 65.4 reduce-scatter.2
